TPU v7x, 32 devices: a whole 2x2x4 slice. The times are simulated.
32 devices in a mesh: blk: 4 (over y, x), half: 2 (over core), rep: 4 (over z).
Axes of the slice: x: 2, y: 2, z: 4, core: 2. Of those that a mesh axis runs over, the one named last changes fastest.
Arguments:
- tokens: bfloat16 [1024, 2048], P('blk'), may hold values from -6 to 6
- experts: int32 [1024, 6], P('blk'), may hold values from 0 to 63, all different within a row; in each aligned block of 256 rows (0 to 255, 256 to 511, ...) at most 32 rows name the same one
- gates: bfloat16 [1024, 6], P('blk'), may hold values from 0.099609375 to 1
- w_gate: bfloat16 [64, 1408, 2048], P('blk', ('half', 'rep')), may hold values from -0.125 to 0.125
- w_up: bfloat16 [64, 1408, 2048], P('blk', ('half', 'rep')), may hold values from -0.125 to 0.125
- w_down: bfloat16 [64, 1408, 2048], P('blk', ('half', 'rep')), may hold values from -0.15625 to 0.15625
- shared_gate: bfloat16 [1408, 2048], P(('half', 'rep')), may hold values from -0.125 to 0.125
- shared_up: bfloat16 [1408, 2048], P(('half', 'rep')), may hold values from -0.125 to 0.125
- shared_down: bfloat16 [1408, 2048], P(('half', 'rep')), may hold values from -0.15625 to 0.15625
Outputs:
- mixed: bfloat16 [1024, 2048], P('blk', ('half', 'rep'))
Inputs may be any that keep to these rules, and one draw needn't show every extreme that they name: Each row names 6 different experts. Among the 256 rows held by one index of blk no expert is named by more than 32 rows, a bound that some block reaches.
All inputs are finite; a program needn't handle non-finite values.
Results may differ from a plain program's by a relative error of at most 0.0055.
Values may be sent and summed in bfloat16 or wider, within the bound.
No kernel may reach another device: no remote copies, remote signals or barrier semaphores. Data moves between devices by JAX's collectives and lax.ppermute only.
A program may use at most 128 MiB of HBM per device.

v0:
```python
import jax
import jax.numpy as jnp
from jax import lax
from jax.sharding import PartitionSpec as P

E = 64
CAP = 32


def hidden_units(token_rows, gate_matrix, up_weight):
    gate_values = jnp.einsum(
        "kan,ktn->kat", token_rows, gate_matrix, preferred_element_type=jnp.float32
    )
    raised_rows = jnp.einsum(
        "kan,ktn->kat", token_rows, up_weight, preferred_element_type=jnp.float32
    )
    return (jax.nn.silu(gate_values) * raised_rows).astype(jnp.bfloat16)


def place_slots(flat, ranks, block_size, which, slot_count):
    inside = ranks // block_size == which
    local = jnp.where(inside, flat * block_size + ranks % block_size, -1)
    return local[:, None] == jnp.arange(slot_count, dtype=jnp.int32)[None, :]


def per_device(tokens, experts, gates, w_gate, w_up, w_down, shared_gate, shared_up, shared_down):
    token_count = tokens.shape[0]
    width = tokens.shape[1]
    topk = experts.shape[1]
    exp_local = w_gate.shape[0]
    blk_count = lax.axis_size("blk")
    slot_block = CAP // lax.axis_size("rep")
    member_rep = lax.axis_index("rep")
    flat = experts.reshape(-1)
    onehot = (flat[:, None] == jnp.arange(E, dtype=jnp.int32)[None, :]).astype(jnp.int32)
    before = jnp.cumsum(onehot, axis=0) - onehot
    ranks = jnp.sum(before * onehot, axis=1)
    placing = place_slots(flat, ranks, slot_block, member_rep, E * slot_block).reshape(
        token_count, topk, -1
    )
    weighting = jnp.sum(
        placing.astype(jnp.float32) * gates.astype(jnp.float32)[:, :, None], axis=1
    ).astype(jnp.bfloat16)
    selector = jnp.any(placing, axis=1).astype(jnp.bfloat16)
    filled = jnp.einsum("ts,td->sd", selector, tokens, preferred_element_type=jnp.float32).astype(
        jnp.bfloat16
    )
    filled = filled.reshape(E, 1, slot_block, width)
    arrived = lax.all_to_all(filled, "blk", split_axis=0, concat_axis=1, tiled=True)
    token_rows = arrived.reshape(exp_local, -1, width)
    every_hidden = hidden_units(lax.all_gather(token_rows, "rep", axis=1, tiled=True), w_gate, w_up)
    mine = lax.all_to_all(every_hidden, "rep", split_axis=1, concat_axis=2, tiled=True)
    partial_value = jnp.einsum(
        "otv,ovj->otj",
        mine,
        lax.all_gather(w_down, "rep", axis=1, tiled=True),
        preferred_element_type=jnp.float32,
    )
    block_out = partial_value.astype(jnp.bfloat16).reshape(exp_local, blk_count, slot_block, width)
    returned = lax.all_to_all(block_out, "blk", split_axis=1, concat_axis=0, tiled=True)
    returned = returned.reshape(E * slot_block, width)
    routed = jnp.dot(weighting, returned, preferred_element_type=jnp.float32)
    shared_hidden = (
        jax.nn.silu(
            jnp.einsum("td,sd->ts", tokens, shared_gate, preferred_element_type=jnp.float32)
        )
        * jnp.einsum("td,sd->ts", tokens, shared_up, preferred_element_type=jnp.float32)
    ).astype(jnp.bfloat16)
    shared_output = jnp.dot(shared_hidden, shared_down, preferred_element_type=jnp.float32)
    routed_share = lax.psum_scatter(routed, ("half", "rep"), scatter_dimension=1, tiled=True)
    shared_share = lax.psum_scatter(shared_output, ("half", "rep"), scatter_dimension=1, tiled=True)
    total = routed_share + shared_share
    return total.astype(jnp.bfloat16)


def solution(mesh):
    return jax.shard_map(
        per_device,
        mesh=mesh,
        in_specs=(
            P("blk", None),
            P("blk", None),
            P("blk", None),
            P("blk", ("half", "rep"), None),
            P("blk", ("half", "rep"), None),
            P("blk", ("half", "rep"), None),
            P(("half", "rep"), None),
            P(("half", "rep"), None),
            P(("half", "rep"), None),
        ),
        out_specs=P("blk", ("half", "rep")),
        check_vma=False,
    )
```

profile of v0, /device:TPU:1, one launch (start us, length us, event | category | flops | bytes accessed | tf_op | source)
XLA Modules:
  0.0 1109.0 jit_solution(772665334566259263)
XLA Ops:
  6.5 0.0 copy-start
  6.5 0.0 copy-start.2
  6.5 0.0 all-gather.3.cloned.1.call-start
  6.5 0.9 copy.61
  7.5 0.1 eq.55
  7.6 0.1 eq.51
  7.8 18.1 %reduce-window.6 = s32[64,12,128]{2,1,0:T(8,128)S(1)} reduce-window(s32[64,12,128]{2,1,0:T(8,128)S(1)} %fusion.6, s32[]{:T(128)} %constant.39.clone.1), window={size=1x1x128 pad=0_0x0_0x127_0}, to_apply=%region_0.0 | reduce-window | flops 12484608 | bytes 786436 | tf_op jit(solution)/shard_map/reduce-window
  25.9 0.2 slice.8
  26.2 0.3 copy.63
  26.5 0.1 copy.64
  26.5 0.2 broadcast_add_fusion
  26.8 0.2 fusion.9
  26.9 0.1 reduce_sum.21
  27.1 0.1 copy.65
  27.2 0.0 copy-done.2
  27.2 0.4 fusion
  27.6 0.0 copy-done
  27.6 0.8 fusion.1
  28.4 28.2 %all_to_all.48 = bf16[64,1,8,2048]{3,2,1,0:T(8,128)(2,1)S(1)} all-to-all(bf16[64,1,8,2048]{3,2,1,0:T(8,128)(2,1)S(1)} %fusion.1), channel_id=1, replica_groups=mesh['blk'=4,'half'=2,'rep'=4] {'blk'}, dimensions={0} | all-to-all | bytes 4194304 | tf_op jit(solution)/shard_map/all_to_all | solution.py:49
  56.6 1.4 copy.79
  58.1 0.0 all-gather.3.cloned.1.call-update
  58.1 0.0 all-gather.5.cloned.1.call-start
  58.1 0.7 all-gather.5.cloned.1.call-update
  58.8 150.4 %all-gather.3.cloned.1.call-done = bf16[16,128,2048]{2,1,0:T(8,128)(2,1)} async-done(((bf16[16,32,2048]{2,1,0:T(8,128)(2,1)}), bf16[16,128,2048]{2,1,0:T(8,128)(2,1)}) %all-gather.3.cloned.1.call-update) | async-done | bytes 8388624 | tf_op jit(solution)/shard_map/all_gather | solution.py:51
  209.2 9.9 fusion.23
  219.1 15.4 %fusion.3 = bf16[16,128,176]{1,2,0:T(8,128)(2,1)S(1)} fusion(bf16[16,128,2048]{2,1,0:T(8,128)(2,1)} %all-gather.3.cloned.1.call-done, bf16[16,176,2048]{2,1,0:T(8,128)(2,1)} %param.13, f32[16,128,176]{1,2,0:T(8,128)S(1)} %fusion.23), kind=kOutput, calls=%fused_computation.10 | convolution fusion | flops 1478557696 | bytes 22085632 | tf_op jit(solution)/shard_map/kan,ktn->kat/dot_general | solution.py:14
  234.5 0.9 copy.71
  235.4 65.3 %all_to_all.49 = bf16[16,128,176]{2,0,1:T(8,128)(2,1)S(1)} all-to-all(bf16[16,128,176]{2,0,1:T(8,128)(2,1)S(1)} %copy.71), channel_id=1, replica_groups=mesh['blk'=4,'half'=2,'rep'=4] {'rep'}, dimensions={1} | all-to-all | bytes 1441792 | tf_op jit(solution)/shard_map/all_to_all | solution.py:52
  300.7 0.8 copy.73
  301.6 1.8 all_to_all.41
  303.3 696.3 %all-gather.5.cloned.1.call-done = bf16[16,704,2048]{2,1,0:T(8,128)(2,1)} async-done(((bf16[16,176,2048]{2,1,0:T(8,128)(2,1)}), bf16[16,704,2048]{2,1,0:T(8,128)(2,1)}) %all-gather.5.cloned.1.call-update) | async-done | bytes 46137360 | tf_op jit(solution)/shard_map/all_gather | solution.py:56
  999.6 18.6 %fusion.2 = bf16[16,4,8,2048]{3,2,1,0:T(8,128)(2,1)S(1)} fusion(bf16[16,32,704]{2,1,0:T(8,128)(2,1)} %all_to_all.41, bf16[16,704,2048]{2,1,0:T(8,128)(2,1)} %all-gather.5.cloned.1.call-done), kind=kOutput, calls=%fused_computation.6 | convolution fusion | flops 1477443584 | bytes 48955392 | tf_op jit(solution)/shard_map/otv,ovj->otj/dot_general | solution.py:53
  1018.3 1.4 copy.74
  1019.7 0.0 copy-start.3
  1019.7 0.0 copy-start.1
  1019.7 4.6 all-to-all-start.2
  1024.3 0.0 reduce-scatter.2.cloned.1.call-start
  1024.3 0.0 copy-done.3
  1024.4 0.6 select_reduce_fusion
  1025.0 0.0 copy-done.1
  1025.0 1.2 fusion.24
  1026.2 2.9 fusion.5
  1029.0 19.7 %all-to-all-done.2 = bf16[16,4,8,2048]{3,2,0,1:T(8,128)(2,1)} async-done(((bf16[16,4,8,2048]{3,2,0,1:T(8,128)(2,1)}), bf16[16,4,8,2048]{3,2,0,1:T(8,128)(2,1)}, u32[]{:S(2)}, u32[]{:S(2)}) %all-to-all-start.2) | async-done | bytes 2097184 | tf_op jit(solution)/shard_map/all_to_all | solution.py:60
  1048.7 3.6 convolution_add_fusion
  1052.3 0.0 reduce-scatter.2.cloned.1.call-update
  1052.4 48.5 %reduce-scatter.2.cloned.1.call-done = f32[256,256]{1,0:T(8,128)} async-done(((f32[256,2048]{1,0:T(8,128)}), f32[256,256]{1,0:T(8,128)}) %reduce-scatter.2.cloned.1.call-update) | async-done | bytes 262160 | tf_op jit(solution)/shard_map/reduce_scatter | solution.py:70
  1100.9 1.6 convert_element_type.38
  (4 shorter events, 0.1 us)
Async XLA Ops:
  6.5 21.1 %copy-start = (bf16[256,2048]{1,0:T(8,128)(2,1)S(1)}, bf16[256,2048]{1,0:T(8,128)(2,1)}, u32[]{:S(2)}) copy-start(bf16[256,2048]{1,0:T(8,128)(2,1)} %param.9) | copy-start | bytes 3145732
  6.5 20.6 %copy-start.2 = (s32[256,6]{0,1:T(8,128)S(1)}, s32[256,6]{0,1:T(8,128)}, u32[]{:S(2)}) copy-start(s32[256,6]{0,1:T(8,128)} %param.10) | copy-start | bytes 18436
  6.5 202.7 %all-gather.3.cloned.1.call-start = ((), (), s32[]{:S(2)}) async-start(), calls=%async_computation.4 | async-start | bytes 10485760 | tf_op jit(solution)/shard_map/all_gather | solution.py:51
  58.1 941.5 %all-gather.5.cloned.1.call-start = ((), (), s32[]{:S(2)}) async-start(), calls=%async_computation.5 | async-start | bytes 57671680 | tf_op jit(solution)/shard_map/all_gather | solution.py:56
  1019.7 4.6 copy-start.3
  1019.7 5.3 copy-start.1
  1019.7 29.0 %all-to-all-start.2 = ((bf16[16,4,8,2048]{3,2,0,1:T(8,128)(2,1)}), bf16[16,4,8,2048]{3,2,0,1:T(8,128)(2,1)}, u32[]{:S(2)}, u32[]{:S(2)}) async-start(bf16[16,4,8,2048]{3,2,0,1:T(8,128)(2,1)} %copy.74), calls=%async_computation.2 | async-start | bytes 4194304 | tf_op jit(solution)/shard_map/all_to_all | solution.py:60
  1024.3 76.6 %reduce-scatter.2.cloned.1.call-start = ((), (), s32[]{:S(2)}) async-start(), calls=%async_computation.6 | async-start | bytes 2359296 | tf_op jit(solution)/shard_map/reduce_scatter | solution.py:70
Sparse Core Ops, SparseCore 0:
  58.2 150.9 all-gather.2
  210.8 788.7 all-gather.4
  1052.5 48.3 reduce-scatter.1
where the time goes:
time: 1110 us
  waiting for transfers between devices  916 us (83%)
  blocking collectives  93.6 us (8%)
  matrix products  52.3 us (5%)
  other arithmetic  21.3 us (2%)
  between operations  13.3 us (1%)
    all_gather x1, waiting for transfers between devices, per_device(): lax.all_gather(w_down, 'rep', axis=1, tiled=True)  696 us
    all_gather x1, waiting for transfers between devices, per_device(): lax.all_gather(token_rows, 'rep', axis=1, tiled=True)  150 us
    all_to_all x1, blocking collectives, per_device(): lax.all_to_all(every_hidden, 'rep', split_axis=1, concat_axis=2, tiled=True)  65.3 us
    reduce_scatter x1, waiting for transfers between devices, per_device(): lax.psum_scatter(routed, ('half', 'rep'), scatter_dimension=1, tiled=True)  48.5 us
    all_to_all x1, blocking collectives, per_device(): lax.all_to_all(filled, 'blk', split_axis=0, concat_axis=1, tiled=True)  28.2 us
  transfers between devices with their start and end apart: 4, of which 4 were waited for; matrix products, arithmetic and copies ran while one was open for 3% of the time, Pallas kernels for 0%

commit v1 on v0

--- a/solution.py
+++ b/solution.py
@@ -5,6 +5,18 @@
 
 E = 64
 CAP = 32
+
+
+def summed_around(value, axis, dim, contribution):
+    devices, mine = (lax.axis_size(axis), lax.axis_index(axis))
+    left = [(i, (i - 1) % devices) for i in range(devices)]
+    rows = value.shape[dim]
+    carried = value
+    total = contribution(carried, mine * rows)
+    for step in range(1, devices):
+        carried = lax.ppermute(carried, axis, left)
+        total = total + contribution(carried, (mine + step) % devices * rows)
+    return total
 
 
 def hidden_units(token_rows, gate_matrix, up_weight):
@@ -50,11 +62,16 @@
     token_rows = arrived.reshape(exp_local, -1, width)
     every_hidden = hidden_units(lax.all_gather(token_rows, "rep", axis=1, tiled=True), w_gate, w_up)
     mine = lax.all_to_all(every_hidden, "rep", split_axis=1, concat_axis=2, tiled=True)
-    partial_value = jnp.einsum(
-        "otv,ovj->otj",
-        mine,
-        lax.all_gather(w_down, "rep", axis=1, tiled=True),
-        preferred_element_type=jnp.float32,
+    partial_value = summed_around(
+        w_down,
+        "rep",
+        1,
+        lambda shard, at: jnp.einsum(
+            "otv,ovj->otj",
+            lax.dynamic_slice_in_dim(mine, at, shard.shape[1], axis=2),
+            shard,
+            preferred_element_type=jnp.float32,
+        ),
     )
     block_out = partial_value.astype(jnp.bfloat16).reshape(exp_local, blk_count, slot_block, width)
     returned = lax.all_to_all(block_out, "blk", split_axis=1, concat_axis=0, tiled=True)

time: 1110 us -> 1040 us (0.937)
  blocking collectives: 93.6 us -> 26.2 us
  waiting for transfers between devices: 916 us -> 895 us
  starting transfers between devices: 4.66 us -> 20.3 us
    all_gather x1 -> x0, waiting for transfers between devices: 696 us -> none  [per_device(): lax.all_gather(w_down, 'rep', axis=1, tiled=True)]
    ppermute x0 -> x3, waiting for transfers between devices: none -> 578 us  [summed_around(): carried = lax.ppermute(carried, axis, left)]
    all_to_all x0 -> x1, waiting for transfers between devices: none -> 241 us  [per_device(): lax.all_to_all(every_hidden, 'rep', split_axis=1, concat_axis=2, tiled=True)]
    all_gather x1, waiting for transfers between devices: 150 us -> 0.01 us  [per_device(): lax.all_gather(token_rows, 'rep', axis=1, tiled=True)]
    all_to_all x1 -> x0, blocking collectives: 65.3 us -> none  [per_device(): lax.all_to_all(every_hidden, 'rep', split_axis=1, concat_axis=2, tiled=True)]
    ppermute x0 -> x3, starting transfers between devices: none -> 12.1 us  [summed_around(): carried = lax.ppermute(carried, axis, left)]
    dot_general x1 -> x4, matrix products: 18.6 us -> 27 us  [per_device(): jnp.einsum('otv,ovj->otj', lax.dynamic_slice_in_dim(mine, at, shard.shape...]
  transfers between devices with their start and end apart: 4 -> 7, of which waited for: 4 -> 5; matrix products, arithmetic and copies ran while one was open for 3% -> 7% of each run, Pallas kernels for 0% -> 0%
where the time goes in v1:
time: 1040 us
  waiting for transfers between devices  895 us (86%)
  matrix products  55.1 us (5%)
  blocking collectives  26.2 us (3%)
  other arithmetic  21.3 us (2%)
  starting transfers between devices  20.3 us (2%)
  between operations  13.6 us (1%)
  local copies, waits for them, and re-layouts  10.4 us (1%)
    ppermute x3, waiting for transfers between devices, summed_around(): carried = lax.ppermute(carried, axis, left)  578 us
    all_to_all x1, waiting for transfers between devices, per_device(): lax.all_to_all(every_hidden, 'rep', split_axis=1, concat_axis=2, tiled=True)  241 us
    reduce_scatter x1, waiting for transfers between devices, per_device(): lax.psum_scatter(routed, ('half', 'rep'), scatter_dimension=1, tiled=True)  55.8 us
    dot_general x4, matrix products, per_device(): jnp.einsum('otv,ovj->otj', lax.dynamic_slice_in_dim(mine, at, shard.shape...  27 us
    all_to_all x1, blocking collectives, per_device(): lax.all_to_all(filled, 'blk', split_axis=0, concat_axis=1, tiled=True)  26.2 us
  transfers between devices with their start and end apart: 7, of which 5 were waited for; matrix products, arithmetic and copies ran while one was open for 7% of the time, Pallas kernels for 0%

profile of v1, /device:TPU:1, one launch (start us, length us, event | category | flops | bytes accessed | tf_op | source)
XLA Modules:
  0.0 1041.8 jit_solution(6342032153191266410)
XLA Ops:
  6.5 0.0 copy-start
  6.5 4.1 collective-permute-start
  10.7 246.9 %collective-permute-done = bf16[16,176,2048]{2,1,0:T(8,128)(2,1)} collective-permute-done((bf16[16,176,2048]{2,1,0:T(8,128)(2,1)}, bf16[16,176,2048]{2,1,0:T(8,128)(2,1)}, u32[]{:S(2)}, u32[]{:S(2)}) %collective-permute-start) | collective-permute-done | bytes 11534368 | tf_op jit(solution)/shard_map/ppermute | solution.py:17
  257.5 4.0 collective-permute-start.1
  261.5 0.8 copy.61
  262.4 0.1 eq.59
  262.5 0.1 eq.55
  262.7 18.1 %reduce-window.6 = s32[64,12,128]{2,1,0:T(8,128)S(1)} reduce-window(s32[64,12,128]{2,1,0:T(8,128)S(1)} %fusion.6, s32[]{:T(128)} %constant.62.clone.1), window={size=1x1x128 pad=0_0x0_0x127_0}, to_apply=%region_0.0 | reduce-window | flops 12484608 | bytes 786436 | tf_op jit(solution)/shard_map/reduce-window
  280.8 0.2 slice.8
  281.1 0.3 copy.63
  281.4 0.1 copy.64
  281.5 0.2 broadcast_add_fusion
  281.7 0.2 fusion.9
  281.9 0.1 reduce_sum.21
  282.0 0.1 copy.65
  282.1 0.4 fusion
  282.6 0.8 fusion.1
  283.3 26.2 %all_to_all.48 = bf16[64,1,8,2048]{3,2,1,0:T(8,128)(2,1)S(1)} all-to-all(bf16[64,1,8,2048]{3,2,1,0:T(8,128)(2,1)S(1)} %fusion.1), channel_id=1, replica_groups=mesh['blk'=4,'half'=2,'rep'=4] {'blk'}, dimensions={0} | all-to-all | bytes 4194304 | tf_op jit(solution)/shard_map/all_to_all | solution.py:61
  309.5 1.5 copy.79
  311.0 0.0 all-gather.2.cloned.1.call-update
  311.0 331.4 %collective-permute-done.1 = bf16[16,176,2048]{2,1,0:T(8,128)(2,1)} collective-permute-done((bf16[16,176,2048]{2,1,0:T(8,128)(2,1)}, bf16[16,176,2048]{2,1,0:T(8,128)(2,1)}, u32[]{:S(2)}, u32[]{:S(2)}) %collective-permute-start.1) | collective-permute-done | bytes 11534368 | tf_op jit(solution)/shard_map/ppermute | solution.py:17
  642.4 4.0 collective-permute-start.2
  646.4 9.8 fusion.34
  656.2 9.8 fusion.3
  666.1 1.7 copy.71
  667.7 3.7 all-to-all-start.1
  671.5 241.0 %all-to-all-done.1 = bf16[16,128,176]{2,0,1:T(8,128)(2,1)S(1)} async-done(((bf16[16,128,176]{2,0,1:T(8,128)(2,1)}), bf16[16,128,176]{2,0,1:T(8,128)(2,1)S(1)}, u32[]{:S(2)}, u32[]{:S(2)}) %all-to-all-start.1) | async-done | bytes 720928 | tf_op jit(solution)/shard_map/all_to_all | solution.py:64
  912.5 1.0 copy-done.1
  913.5 2.0 copy.73
  915.5 0.9 all_to_all.41
  916.5 6.7 fusion.15
  923.1 6.7 fusion.13
  929.8 6.7 fusion.11
  936.4 0.0 collective-permute-done.2
  936.4 7.1 fusion.2
  943.5 0.0 copy-start.4
  943.5 0.0 copy-start.2
  943.6 1.4 copy.74
  945.0 4.4 all-to-all-start.2
  949.4 0.0 reduce-scatter.2.cloned.1.call-start
  949.5 0.6 select_reduce_fusion
  950.2 1.2 fusion.35
  951.3 2.9 fusion.5
  954.2 19.7 %all-to-all-done.2 = bf16[16,4,8,2048]{3,2,0,1:T(8,128)(2,1)} async-done(((bf16[16,4,8,2048]{3,2,0,1:T(8,128)(2,1)}), bf16[16,4,8,2048]{3,2,0,1:T(8,128)(2,1)}, u32[]{:S(2)}, u32[]{:S(2)}) %all-to-all-start.2) | async-done | bytes 2097184 | tf_op jit(solution)/shard_map/all_to_all | solution.py:77
  973.9 3.6 convolution_add_fusion
  977.5 0.0 reduce-scatter.2.cloned.1.call-update
  977.5 55.8 %reduce-scatter.2.cloned.1.call-done = f32[256,256]{1,0:T(8,128)} async-done(((f32[256,2048]{1,0:T(8,128)}), f32[256,256]{1,0:T(8,128)}) %reduce-scatter.2.cloned.1.call-update) | async-done | bytes 262160 | tf_op jit(solution)/shard_map/reduce_scatter | solution.py:87
  1033.3 1.6 convert_element_type.38
  (12 shorter events, 0.1 us)
Async XLA Ops:
  6.5 276.0 %copy-start = (bf16[256,2048]{1,0:T(8,128)(2,1)S(1)}, bf16[256,2048]{1,0:T(8,128)(2,1)}, u32[]{:S(2)}) copy-start(bf16[256,2048]{1,0:T(8,128)(2,1)} %param.9) | copy-start | bytes 3145732
  6.5 275.5 %copy-start.3 = (s32[256,6]{0,1:T(8,128)S(1)}, s32[256,6]{0,1:T(8,128)}, u32[]{:S(2)}) copy-start(s32[256,6]{0,1:T(8,128)} %param.10) | copy-start | bytes 18436
  6.5 639.9 %all-gather.2.cloned.1.call-start = ((), (), s32[]{:S(2)}) async-start(), calls=%async_computation.4 | async-start | bytes 10485760 | tf_op jit(solution)/shard_map/all_gather | solution.py:63
  6.5 251.0 %collective-permute-start = (bf16[16,176,2048]{2,1,0:T(8,128)(2,1)}, bf16[16,176,2048]{2,1,0:T(8,128)(2,1)}, u32[]{:S(2)}, u32[]{:S(2)}) collective-permute-start(bf16[16,176,2048]{2,1,0:T(8,128)(2,1)} %param.14), channel_id=1, source_target_pairs={{0,3},{1,0},{2,1},{3,2},{4,7},{5,4},{6,5},{7,6},{8,11},{9,8},{10,9... | collective-permute-start | bytes 34603016 | tf_op jit(solution)/shard_map/ppermute | solution.py:17
  257.5 384.9 %collective-permute-start.1 = (bf16[16,176,2048]{2,1,0:T(8,128)(2,1)}, bf16[16,176,2048]{2,1,0:T(8,128)(2,1)}, u32[]{:S(2)}, u32[]{:S(2)}) collective-permute-start(bf16[16,176,2048]{2,1,0:T(8,128)(2,1)} %collective-permute-done), channel_id=1, source_target_pairs={{0,3},{1,0},{2,1},{3,2},{4,7},{5,4},{6,5},{7,6},{8,11},{9,8},{10,9... | collective-permute-start | bytes 34603016 | tf_op jit(solution)/shard_map/ppermute | solution.py:17
  642.4 294.0 %collective-permute-start.2 = (bf16[16,176,2048]{2,1,0:T(8,128)(2,1)}, bf16[16,176,2048]{2,1,0:T(8,128)(2,1)}, u32[]{:S(2)}, u32[]{:S(2)}) collective-permute-start(bf16[16,176,2048]{2,1,0:T(8,128)(2,1)} %collective-permute-done.1), channel_id=1, source_target_pairs={{0,3},{1,0},{2,1},{3,2},{4,7},{5,4},{6,5},{7,6},{8,11},{9,8},{10,9... | collective-permute-start | bytes 34603016 | tf_op jit(solution)/shard_map/ppermute | solution.py:17
  667.7 244.8 %all-to-all-start.1 = ((bf16[16,128,176]{2,0,1:T(8,128)(2,1)}), bf16[16,128,176]{2,0,1:T(8,128)(2,1)S(1)}, u32[]{:S(2)}, u32[]{:S(2)}) async-start(bf16[16,128,176]{2,0,1:T(8,128)(2,1)} %copy.71), calls=%async_computation.1 | async-start | bytes 2097152 | tf_op jit(solution)/shard_map/all_to_all | solution.py:64
  912.5 1.0 copy-start.1
  943.5 6.0 copy-start.4
  943.5 6.6 copy-start.2
  945.0 28.9 %all-to-all-start.2 = ((bf16[16,4,8,2048]{3,2,0,1:T(8,128)(2,1)}), bf16[16,4,8,2048]{3,2,0,1:T(8,128)(2,1)}, u32[]{:S(2)}, u32[]{:S(2)}) async-start(bf16[16,4,8,2048]{3,2,0,1:T(8,128)(2,1)} %copy.74), calls=%async_computation.2 | async-start | bytes 4194304 | tf_op jit(solution)/shard_map/all_to_all | solution.py:77
  949.4 83.9 %reduce-scatter.2.cloned.1.call-start = ((), (), s32[]{:S(2)}) async-start(), calls=%async_computation.5 | async-start | bytes 2359296 | tf_op jit(solution)/shard_map/reduce_scatter | solution.py:87
Sparse Core Ops, SparseCore 0:
  311.1 279.3 all-gather.1
  977.6 55.6 reduce-scatter.1
